TPU v7x, 128 devices: a whole 4x4x4 slice. The times are simulated.
128 devices in a mesh: dom: 4 (over y_hi, core), dim: 32 (over z, y_lo, x).
Axes of the slice: x: 4, y: 4 (y_hi: 2, y_lo: 2; y = y_hi * 2 + y_lo), z: 4, core: 2. Of those that a mesh axis runs over, the one named last changes fastest.
Arguments:
- particles: float32 [512, 262144], P('dom', 'dim'), may hold values from -16 to 16
- scores: float32 [512, 262144], P('dom', 'dim'), may hold values from -0.00036621094 to 0.00036621094
- spread: float32 [], replicated, may hold values from 131072 to 262144
- step_size: float32 [], replicated, may hold values from 4194304 to 8388608
Outputs:
- new_particles: float32 [512, 262144], P('dom', 'dim')
All inputs are finite; a program needn't handle non-finite values.
Results may differ from a plain program's by a relative error of at most 0.000064.
Values sent between devices are 32-bit elements; how exact they have to be, the bound alone decides.
A program may use at most 128 MiB of HBM per device.

v0:
```python
import jax
import jax.numpy as jnp
from jax import lax
from jax.sharding import PartitionSpec as P


def cut_along(array, dim, devices):
    dims = array.shape
    blocks = array.reshape(*dims[:dim], devices, dims[dim] // devices, *dims[dim + 1 :])
    return jnp.moveaxis(blocks, dim, 0)


def sum_at_owner(array, axis, dim):
    blocks = cut_along(array, dim, lax.axis_size(axis))
    arrived = lax.all_to_all(blocks, axis, split_axis=0, concat_axis=0, tiled=True)
    return arrived.sum(axis=0)


def from_everyone(array, axis):
    devices = lax.axis_size(axis)
    return lax.all_to_all(
        jnp.broadcast_to(array[None], (devices, *array.shape)), axis, 0, 0, tiled=True
    )


def over_copies(array, axis):
    everything = from_everyone(array, axis)
    return jnp.sum(everything, axis=0)


def in_order(blocks, dim):
    dims = list(blocks.shape[1:])
    dims[dim] *= blocks.shape[0]
    return jnp.moveaxis(blocks, 0, dim).reshape(dims)


def gathered_copies(array, axis, dim):
    return in_order(from_everyone(array, axis), dim)


def on_device(particles, scores, spread, step_size):
    precise = lax.Precision.HIGHEST
    local_rows = particles.shape[0]
    count_all = local_rows * lax.axis_size("dom")
    gathered = lax.all_gather(particles, "dom", axis=0, tiled=True)
    product = lax.dot_general(
        particles,
        gathered,
        (((1,), (1,)), ((), ())),
        precision=precise,
        preferred_element_type=jnp.float32,
    )
    norms = jnp.sum(gathered * gathered, axis=1)
    gram_share, square_share = (sum_at_owner(product, "dim", 1), sum_at_owner(norms, "dim", 0))
    own_squares = over_copies(jnp.sum(particles * particles, axis=1), "dim")
    kernel_share = jnp.exp(
        -(own_squares[:, None] + square_share[None, :] - 2.0 * gram_share) / spread
    )
    kernel = gathered_copies(kernel_share, "dim", 1)
    attract = jnp.dot(
        kernel,
        lax.all_gather(scores, "dom", axis=0, tiled=True),
        precision=precise,
        preferred_element_type=jnp.float32,
    )
    pulled = jnp.dot(kernel, gathered, precision=precise, preferred_element_type=jnp.float32)
    weight_sum = jnp.sum(kernel, axis=1, keepdims=True)
    update = (attract + 2.0 / spread * (weight_sum * particles - pulled)) / count_all
    return particles + step_size * update


def solution(mesh):
    return jax.shard_map(
        on_device,
        mesh=mesh,
        in_specs=(P("dom", "dim"), P("dom", "dim"), P(), P()),
        out_specs=P("dom", "dim"),
        check_vma=False,
    )
```

profile of v0, /device:TPU:1, one launch (start us, length us, event | category | flops | bytes accessed | tf_op | source)
XLA Modules:
  0.0 261.2 jit_solution(14739660811756581120)
XLA Ops:
  6.5 0.0 all-gather.3.cloned.1.call-start
  6.5 0.7 all-gather.3.cloned.1.call-update
  7.3 0.0 all-gather.5.cloned.1.call-start
  7.3 0.7 all-gather.5.cloned.1.call-update
  8.0 2.5 multiply_reduce_fusion.1
  10.5 0.6 broadcast_in_dim.4
  11.2 9.7 %all-to-all-start = ((f32[32,1,128]{2,1,0:T(1,128)}), f32[32,1,128]{2,1,0:T(1,128)S(1)}, u32[]{:S(2)}, u32[]{:S(2)}) async-start(f32[32,1,128]{2,1,0:T(1,128)} %broadcast_in_dim.4), calls=%async_computation | async-start | bytes 32768 | tf_op jit(solution)/shard_map/all_to_all | solution.py:21
  20.9 101.7 %all-gather.3.cloned.1.call-done = f32[512,8192]{1,0:T(8,128)} async-done(((f32[128,8192]{1,0:T(8,128)}), f32[512,8192]{1,0:T(8,128)}) %all-gather.3.cloned.1.call-update) | async-done | bytes 16777232 | tf_op jit(solution)/shard_map/all_gather | solution.py:45
  122.6 7.0 %multiply_reduce_fusion = f32[512]{0:T(512)S(1)} fusion(f32[512,8192]{1,0:T(8,128)} %all-gather.3.cloned.1.call-done), kind=kLoop, calls=%fused_computation | loop fusion | flops 8388096 | bytes 16779264 | tf_op jit(solution)/shard_map/reduce_sum | solution.py:53
  129.6 0.7 all_to_all.17
  130.2 0.0 all-to-all-done
  130.2 7.0 %all-to-all-start.1 = ((f32[32,1,16]{2,1,0:T(1,128)}), f32[32,1,16]{2,1,0:T(1,128)S(1)}, u32[]{:S(2)}, u32[]{:S(2)}) async-start(f32[32,1,16]{2,1,0:T(1,128)} %bitcast.1), calls=%async_computation.1 | async-start | bytes 32768 | tf_op jit(solution)/shard_map/all_to_all | solution.py:15
  137.2 17.7 %fusion.3 = f32[128,512]{0,1:T(8,128)} fusion(f32[128,8192]{1,0:T(8,128)} %param.4, f32[512,8192]{1,0:T(8,128)} %all-gather.3.cloned.1.call-done), kind=kOutput, calls=%fused_computation.8 | convolution fusion | flops 6442450944 | bytes 21233664 | tf_op jit(solution)/shard_map/dot_general | solution.py:46
  155.0 0.0 all-to-all-done.1
  155.0 7.8 %all-to-all-start.2 = ((f32[32,128,16]{1,2,0:T(8,128)}), f32[32,128,16]{1,2,0:T(8,128)S(1)}, u32[]{:S(2)}, u32[]{:S(2)}) async-start(f32[32,128,16]{1,2,0:T(8,128)} %bitcast.3), calls=%async_computation.2 | async-start | bytes 524288 | tf_op jit(solution)/shard_map/all_to_all | solution.py:15
  163.4 0.1 reduce_sum.57
  163.5 7.5 %all-to-all-done.2 = f32[32,128,16]{1,2,0:T(8,128)S(1)} async-done(((f32[32,128,16]{1,2,0:T(8,128)}), f32[32,128,16]{1,2,0:T(8,128)S(1)}, u32[]{:S(2)}, u32[]{:S(2)}) %all-to-all-start.2) | async-done | bytes 262176 | tf_op jit(solution)/shard_map/all_to_all | solution.py:15
  171.0 0.1 divide_exponential_fusion
  171.1 0.7 broadcast_in_dim.5
  171.8 5.5 %all-to-all-start.3 = ((f32[32,128,16]{1,2,0:T(8,128)}), f32[32,128,16]{1,2,0:T(8,128)S(1)}, u32[]{:S(2)}, u32[]{:S(2)}) async-start(f32[32,128,16]{1,2,0:T(8,128)} %broadcast_in_dim.5), calls=%async_computation.3 | async-start | bytes 524288 | tf_op jit(solution)/shard_map/all_to_all | solution.py:21
  178.0 7.3 %all-to-all-done.3 = f32[32,128,16]{1,2,0:T(8,128)S(1)} async-done(((f32[32,128,16]{1,2,0:T(8,128)}), f32[32,128,16]{1,2,0:T(8,128)S(1)}, u32[]{:S(2)}, u32[]{:S(2)}) %all-to-all-start.3) | async-done | bytes 262176 | tf_op jit(solution)/shard_map/all_to_all | solution.py:21
  185.4 0.1 reduce_sum.59
  185.4 14.4 %fusion = f32[128,8192]{1,0:T(8,128)} fusion(f32[128,512]{0,1:T(8,128)S(1)} %bitcast.14, f32[512,8192]{1,0:T(8,128)} %all-gather.3.cloned.1.call-done, f32[128,8192]{1,0:T(8,128)} %param.4, f32[128]{0:T(128)S(1)} %reduce_sum.59, f32[]{:T(128)S(6)} %div.17), kind=kOutput, calls=%fused_computation.2 | convolution fusion | flops 6445596672 | bytes 25428484 | tf_op jit(solution)/shard_map/dot_general | solution.py:66
  199.8 39.6 %all-gather.5.cloned.1.call-done = f32[512,8192]{1,0:T(8,128)} async-done(((f32[128,8192]{1,0:T(8,128)}), f32[512,8192]{1,0:T(8,128)}) %all-gather.5.cloned.1.call-update) | async-done | bytes 16777232 | tf_op jit(solution)/shard_map/all_gather | solution.py:62
  239.4 15.0 %fusion.2 = f32[128,8192]{1,0:T(8,128)} fusion(f32[128,8192]{1,0:T(8,128)} %param.4, f32[128,8192]{1,0:T(8,128)} %fusion, f32[128,512]{0,1:T(8,128)S(1)} %bitcast.15, f32[512,8192]{1,0:T(8,128)} %all-gather.5.cloned.1.call-done, f32[]{:T(128)S(6)} %mul.46), kind=kOutput, calls=%fused_computation.5 | convolution fusion | flops 6445596672 | bytes 29622276 | tf_op jit(solution)/shard_map/dot_general | solution.py:60
  (2 shorter events, 0.1 us)
Async XLA Ops:
  6.5 116.1 %all-gather.3.cloned.1.call-start = ((), (), s32[]{:S(2)}) async-start(), calls=%async_computation.4 | async-start | bytes 20971520 | tf_op jit(solution)/shard_map/all_gather | solution.py:45
  7.3 232.1 %all-gather.5.cloned.1.call-start = ((), (), s32[]{:S(2)}) async-start(), calls=%async_computation.5 | async-start | bytes 20971520 | tf_op jit(solution)/shard_map/all_gather | solution.py:62
  11.2 119.1 %all-to-all-start = ((f32[32,1,128]{2,1,0:T(1,128)}), f32[32,1,128]{2,1,0:T(1,128)S(1)}, u32[]{:S(2)}, u32[]{:S(2)}) async-start(f32[32,1,128]{2,1,0:T(1,128)} %broadcast_in_dim.4), calls=%async_computation | async-start | bytes 32768 | tf_op jit(solution)/shard_map/all_to_all | solution.py:21
  130.2 24.7 %all-to-all-start.1 = ((f32[32,1,16]{2,1,0:T(1,128)}), f32[32,1,16]{2,1,0:T(1,128)S(1)}, u32[]{:S(2)}, u32[]{:S(2)}) async-start(f32[32,1,16]{2,1,0:T(1,128)} %bitcast.1), calls=%async_computation.1 | async-start | bytes 32768 | tf_op jit(solution)/shard_map/all_to_all | solution.py:15
  155.0 16.0 %all-to-all-start.2 = ((f32[32,128,16]{1,2,0:T(8,128)}), f32[32,128,16]{1,2,0:T(8,128)S(1)}, u32[]{:S(2)}, u32[]{:S(2)}) async-start(f32[32,128,16]{1,2,0:T(8,128)} %bitcast.3), calls=%async_computation.2 | async-start | bytes 524288 | tf_op jit(solution)/shard_map/all_to_all | solution.py:15
  171.8 13.5 %all-to-all-start.3 = ((f32[32,128,16]{1,2,0:T(8,128)}), f32[32,128,16]{1,2,0:T(8,128)S(1)}, u32[]{:S(2)}, u32[]{:S(2)}) async-start(f32[32,128,16]{1,2,0:T(8,128)} %broadcast_in_dim.5), calls=%async_computation.3 | async-start | bytes 524288 | tf_op jit(solution)/shard_map/all_to_all | solution.py:21
Sparse Core Ops, SparseCore 0:
  9.0 113.5 all-gather.2
  124.3 115.0 all-gather.4
where the time goes:
time: 262 us; the launch traced here: 261 us
  waiting for transfers between devices  157 us (60%)
  matrix products  47.1 us (18%)
  starting transfers between devices  30 us (11%)
  between operations  14.8 us (6%)
  other arithmetic  9.76 us (4%)
    all_gather x1, waiting for transfers between devices, on_device(): gathered = lax.all_gather(particles, 'dom', axis=0, tiled=True)  102 us
    all_gather x1, waiting for transfers between devices, on_device(): lax.all_gather(scores, 'dom', axis=0, tiled=True)  39.6 us
    dot_general x1, matrix products, on_device(): lax.dot_general(particles, gathered, (((1,), (1,)), ((), ())), precision=...  17.7 us
    all_to_all x2, starting transfers between devices, from_everyone(): lax.all_to_all(jnp.broadcast_to(array[None], (devices, *array.shape)), ax...  15.2 us
    dot_general x1, matrix products, on_device(): jnp.dot(kernel, lax.all_gather(scores, 'dom', axis=0, tiled=True), precis...  15 us
    all_to_all x2, starting transfers between devices, sum_at_owner(): lax.all_to_all(blocks, axis, split_axis=0, concat_axis=0, tiled=True)  14.8 us
    dot_general x1, matrix products, on_device(): jnp.dot(kernel, gathered, precision=precise, preferred_element_type=jnp.f...  14.4 us
    all_to_all x2, waiting for transfers between devices, sum_at_owner(): lax.all_to_all(blocks, axis, split_axis=0, concat_axis=0, tiled=True)  7.48 us
  transfers between devices with their start and end apart: 6, of which 4 were waited for; matrix products, arithmetic and copies ran while one was open for 17% of the time, Pallas kernels for 0%

commit v1 on v0

--- a/solution.py
+++ b/solution.py
@@ -2,6 +2,12 @@
 import jax.numpy as jnp
 from jax import lax
 from jax.sharding import PartitionSpec as P
+
+
+def run_points_on(dim_no, my_tile):
+    w1 = jnp.stack([my_tile for _ in range(lax.axis_size("dom"))])
+    part_next = jnp.concatenate(lax.all_to_all(w1, "dom", 0, 0), dim_no)
+    return part_next
 
 
 def cut_along(array, dim, devices):
@@ -58,10 +64,7 @@
     )
     kernel = gathered_copies(kernel_share, "dim", 1)
     attract = jnp.dot(
-        kernel,
-        lax.all_gather(scores, "dom", axis=0, tiled=True),
-        precision=precise,
-        preferred_element_type=jnp.float32,
+        kernel, run_points_on(0, scores), precision=precise, preferred_element_type=jnp.float32
     )
     pulled = jnp.dot(kernel, gathered, precision=precise, preferred_element_type=jnp.float32)
     weight_sum = jnp.sum(kernel, axis=1, keepdims=True)

time: 262 us -> 408 us (1.56)
  waiting for transfers between devices: 157 us -> 279 us
  blocking collectives: 0 us -> 11.7 us
  local copies, waits for them, and re-layouts: 2.04 us -> 11.2 us
  starting transfers between devices: 30 us -> 34.6 us
    all_to_all x0 -> x1, waiting for transfers between devices: none -> 168 us  [run_points_on(): part_next = jnp.concatenate(lax.all_to_all(w1, 'dom', 0, 0), dim_no)]
    all_gather x1 -> x0, waiting for transfers between devices: 39.6 us -> none  [on_device(): lax.all_gather(scores, 'dom', axis=0, tiled=True)]
    all_to_all x0 -> x1, blocking collectives: none -> 11.7 us  [from_everyone(): lax.all_to_all(jnp.broadcast_to(array[None], (devices, *array.shape)), ax...]
    all_to_all x0 -> x1, starting transfers between devices: none -> 10.2 us  [run_points_on(): part_next = jnp.concatenate(lax.all_to_all(w1, 'dom', 0, 0), dim_no)]
    another operation x0 -> x1, local copies, waits for them, and re-layouts: none -> 9.91 us  [run_points_on(): w1 = jnp.stack([my_tile for _ in range(lax.axis_size('dom'))])]
    all_to_all x2 -> x1, waiting for transfers between devices: 7.32 us -> 0.01 us  [from_everyone(): lax.all_to_all(jnp.broadcast_to(array[None], (devices, *array.shape)), ax...]
    all_to_all x2 -> x1, starting transfers between devices: 15.2 us -> 9.71 us  [from_everyone(): lax.all_to_all(jnp.broadcast_to(array[None], (devices, *array.shape)), ax...]
  transfers between devices with their start and end apart: 6 -> 5, of which waited for: 4 -> 3; matrix products, arithmetic and copies ran while one was open for 17% -> 10% of each run, Pallas kernels for 0% -> 0%
where the time goes in v1:
time: 408 us
  waiting for transfers between devices  279 us (68%)
  matrix products  46.3 us (11%)
  starting transfers between devices  34.6 us (8%)
  between operations  14.8 us (4%)
  blocking collectives  11.7 us (3%)
  local copies, waits for them, and re-layouts  11.2 us (3%)
  other arithmetic  9.76 us (2%)
    all_to_all x1, waiting for transfers between devices, run_points_on(): part_next = jnp.concatenate(lax.all_to_all(w1, 'dom', 0, 0), dim_no)  168 us
    all_gather x1, waiting for transfers between devices, on_device(): gathered = lax.all_gather(particles, 'dom', axis=0, tiled=True)  102 us
    dot_general x1, matrix products, on_device(): lax.dot_general(particles, gathered, (((1,), (1,)), ((), ())), precision=...  16.9 us
    dot_general x1, matrix products, on_device(): jnp.dot(kernel, run_points_on(0, scores), precision=precise, preferred_el...  15 us
    all_to_all x2, starting transfers between devices, sum_at_owner(): lax.all_to_all(blocks, axis, split_axis=0, concat_axis=0, tiled=True)  14.7 us
    dot_general x1, matrix products, on_device(): jnp.dot(kernel, gathered, precision=precise, preferred_element_type=jnp.f...  14.4 us
    all_to_all x1, blocking collectives, from_everyone(): lax.all_to_all(jnp.broadcast_to(array[None], (devices, *array.shape)), ax...  11.7 us
    all_to_all x1, starting transfers between devices, run_points_on(): part_next = jnp.concatenate(lax.all_to_all(w1, 'dom', 0, 0), dim_no)  10.2 us
  transfers between devices with their start and end apart: 5, of which 3 were waited for; matrix products, arithmetic and copies ran while one was open for 10% of the time, Pallas kernels for 0%

profile of v1, /device:TPU:1, one launch (start us, length us, event | category | flops | bytes accessed | tf_op | source)
XLA Modules:
  0.0 407.5 jit_solution(8494197300338567674)
XLA Ops:
  6.5 0.0 all-gather.2.cloned.1.call-start
  6.5 0.7 all-gather.2.cloned.1.call-update
  7.3 2.5 multiply_reduce_fusion.1
  9.8 0.6 broadcast_in_dim.4
  10.4 9.7 %all-to-all-start = ((f32[32,1,128]{2,1,0:T(1,128)}), f32[32,1,128]{2,1,0:T(1,128)S(1)}, u32[]{:S(2)}, u32[]{:S(2)}) async-start(f32[32,1,128]{2,1,0:T(1,128)} %broadcast_in_dim.4), calls=%async_computation | async-start | bytes 32768 | tf_op jit(solution)/shard_map/all_to_all | solution.py:27
  20.1 102.4 %all-gather.2.cloned.1.call-done = f32[512,8192]{1,0:T(8,128)} async-done(((f32[128,8192]{1,0:T(8,128)}), f32[512,8192]{1,0:T(8,128)}) %all-gather.2.cloned.1.call-update) | async-done | bytes 16777232 | tf_op jit(solution)/shard_map/all_gather | solution.py:51
  122.6 7.0 %multiply_reduce_fusion = f32[512]{0:T(512)S(1)} fusion(f32[512,8192]{1,0:T(8,128)} %all-gather.2.cloned.1.call-done), kind=kLoop, calls=%fused_computation | loop fusion | flops 8388096 | bytes 16779264 | tf_op jit(solution)/shard_map/reduce_sum | solution.py:59
  129.6 0.7 all_to_all.20
  130.2 0.0 all-to-all-done
  130.2 7.0 %all-to-all-start.1 = ((f32[32,1,16]{2,1,0:T(1,128)}), f32[32,1,16]{2,1,0:T(1,128)S(1)}, u32[]{:S(2)}, u32[]{:S(2)}) async-start(f32[32,1,16]{2,1,0:T(1,128)} %bitcast.1), calls=%async_computation.1 | async-start | bytes 32768 | tf_op jit(solution)/shard_map/all_to_all | solution.py:21
  137.2 16.9 %fusion.3 = f32[128,512]{0,1:T(8,128)} fusion(f32[128,8192]{1,0:T(8,128)} %param.4, f32[512,8192]{1,0:T(8,128)} %all-gather.2.cloned.1.call-done), kind=kOutput, calls=%fused_computation.8 | convolution fusion | flops 6442450944 | bytes 21233664 | tf_op jit(solution)/shard_map/dot_general | solution.py:52
  154.2 0.0 all-to-all-done.1
  154.2 7.7 %all-to-all-start.2 = ((f32[32,128,16]{1,2,0:T(8,128)}), f32[32,128,16]{1,2,0:T(8,128)S(1)}, u32[]{:S(2)}, u32[]{:S(2)}) async-start(f32[32,128,16]{1,2,0:T(8,128)} %bitcast.3), calls=%async_computation.2 | async-start | bytes 524288 | tf_op jit(solution)/shard_map/all_to_all | solution.py:21
  162.6 0.1 reduce_sum.57
  162.6 7.5 %all-to-all-done.2 = f32[32,128,16]{1,2,0:T(8,128)S(1)} async-done(((f32[32,128,16]{1,2,0:T(8,128)}), f32[32,128,16]{1,2,0:T(8,128)S(1)}, u32[]{:S(2)}, u32[]{:S(2)}) %all-to-all-start.2) | async-done | bytes 262176 | tf_op jit(solution)/shard_map/all_to_all | solution.py:21
  170.1 0.1 divide_exponential_fusion
  170.2 11.7 %all_to_all.30 = f32[32,128,16]{1,2,0:T(8,128)S(1)} all-to-all(f32[32,128,16]{1,2,0:T(8,128)S(1)} %broadcast_in_dim.5), channel_id=1, replica_groups=mesh['dom'=4,'dim'=32] {'dim'}, dimensions={0} | all-to-all | bytes 524288 | tf_op jit(solution)/shard_map/all_to_all | solution.py:27
  181.9 9.9 %stack.2 = f32[4,128,8192]{2,1,0:T(8,128)} broadcast(f32[128,8192]{1,0:T(8,128)} %param.5), dimensions={1,2} | broadcast | bytes 20971520 | tf_op jit(solution)/shard_map/stack | solution.py:8
  191.9 10.2 %all-to-all-start.4 = ((f32[4,128,8192]{2,1,0:T(8,128)}), f32[4,128,8192]{2,1,0:T(8,128)}, u32[]{:S(2)}, u32[]{:S(2)}) async-start(f32[4,128,8192]{2,1,0:T(8,128)} %stack.2), calls=%async_computation.4 | async-start | bytes 33554432 | tf_op jit(solution)/shard_map/all_to_all | solution.py:9
  202.8 0.1 reduce_sum.59
  202.8 14.4 %fusion = f32[128,8192]{1,0:T(8,128)} fusion(f32[128,512]{0,1:T(8,128)S(1)} %bitcast.15, f32[512,8192]{1,0:T(8,128)} %all-gather.2.cloned.1.call-done, f32[128,8192]{1,0:T(8,128)} %param.4, f32[128]{0:T(128)S(1)} %reduce_sum.59, f32[]{:T(128)S(6)} %div.17), kind=kOutput, calls=%fused_computation.2 | convolution fusion | flops 6445596672 | bytes 25428484 | tf_op jit(solution)/shard_map/dot_general | solution.py:69
  217.2 168.4 %all-to-all-done.4 = f32[4,128,8192]{2,1,0:T(8,128)} async-done(((f32[4,128,8192]{2,1,0:T(8,128)}), f32[4,128,8192]{2,1,0:T(8,128)}, u32[]{:S(2)}, u32[]{:S(2)}) %all-to-all-start.4) | async-done | bytes 16777248 | tf_op jit(solution)/shard_map/all_to_all | solution.py:9
  385.7 15.0 %fusion.2 = f32[128,8192]{1,0:T(8,128)} fusion(f32[128,8192]{1,0:T(8,128)} %param.4, f32[128,8192]{1,0:T(8,128)} %fusion, f32[128,512]{0,1:T(8,128)S(1)} %bitcast.16, f32[512,8192]{1,0:T(8,128)} %bitcast.6, f32[]{:T(128)S(6)} %mul.46), kind=kOutput, calls=%fused_computation.5 | convolution fusion | flops 6445596672 | bytes 29622276 | tf_op jit(solution)/shard_map/dot_general | solution.py:66
  (3 shorter events, 0.1 us)
Async XLA Ops:
  6.5 116.1 %all-gather.2.cloned.1.call-start = ((), (), s32[]{:S(2)}) async-start(), calls=%async_computation.5 | async-start | bytes 20971520 | tf_op jit(solution)/shard_map/all_gather | solution.py:51
  10.4 119.8 %all-to-all-start = ((f32[32,1,128]{2,1,0:T(1,128)}), f32[32,1,128]{2,1,0:T(1,128)S(1)}, u32[]{:S(2)}, u32[]{:S(2)}) async-start(f32[32,1,128]{2,1,0:T(1,128)} %broadcast_in_dim.4), calls=%async_computation | async-start | bytes 32768 | tf_op jit(solution)/shard_map/all_to_all | solution.py:27
  130.2 23.9 %all-to-all-start.1 = ((f32[32,1,16]{2,1,0:T(1,128)}), f32[32,1,16]{2,1,0:T(1,128)S(1)}, u32[]{:S(2)}, u32[]{:S(2)}) async-start(f32[32,1,16]{2,1,0:T(1,128)} %bitcast.1), calls=%async_computation.1 | async-start | bytes 32768 | tf_op jit(solution)/shard_map/all_to_all | solution.py:21
  154.2 15.9 %all-to-all-start.2 = ((f32[32,128,16]{1,2,0:T(8,128)}), f32[32,128,16]{1,2,0:T(8,128)S(1)}, u32[]{:S(2)}, u32[]{:S(2)}) async-start(f32[32,128,16]{1,2,0:T(8,128)} %bitcast.3), calls=%async_computation.2 | async-start | bytes 524288 | tf_op jit(solution)/shard_map/all_to_all | solution.py:21
  191.9 193.8 %all-to-all-start.4 = ((f32[4,128,8192]{2,1,0:T(8,128)}), f32[4,128,8192]{2,1,0:T(8,128)}, u32[]{:S(2)}, u32[]{:S(2)}) async-start(f32[4,128,8192]{2,1,0:T(8,128)} %stack.2), calls=%async_computation.4 | async-start | bytes 33554432 | tf_op jit(solution)/shard_map/all_to_all | solution.py:9
Sparse Core Ops, SparseCore 0:
  9.0 113.5 all-gather.1
